TPU v7x, 32 devices: a whole 2x2x4 slice. The times are simulated.
32 devices in a mesh: wide: 16 (over z, y, x), narrow: 2 (over core).
Axes of the slice: x: 2, y: 2, z: 4, core: 2. Of those that a mesh axis runs over, the one named last changes fastest.
Arguments:
- node_latent: bfloat16 [4096, 512], P(('wide', 'narrow')), may hold values from -6 to 6
- edge_latent: bfloat16 [16384, 512], P(('wide', 'narrow')), may hold values from -6 to 6
- node_cotangent: bfloat16 [4096, 512], P(('wide', 'narrow')), may hold values from -6 to 6
- w_first: bfloat16 [1536, 512], replicated, may hold values from -2 to 2
- bias_first: bfloat16 [512], replicated, may hold values from -4 to 4
- w_second: bfloat16 [512, 512], replicated, may hold values from -2 to 2
- bias_second: bfloat16 [512], replicated, may hold values from -4 to 4
- norm_gain: bfloat16 [512], replicated, may hold values from 0.099609375 to 1.8984375
- send_map: int32 [32, 4, 64], P(('wide', 'narrow')), may hold values from -1 to 127, as said below
- edge_sender: int32 [16384], P(('wide', 'narrow')), may hold values from 0 to 383, as said below
- edge_receiver: int32 [16384], P(('wide', 'narrow')), may hold values from 0 to 127
Outputs:
- node_grad: bfloat16 [4096, 512], P(('wide', 'narrow'))
- edge_grad: bfloat16 [16384, 512], P(('wide', 'narrow'))
- first_update: float32 [1536, 512], P('wide')
- second_update: float32 [512, 512], P('wide')
Inputs may be any that keep to these rules, and one draw needn't show every extreme that they name: `send_map`: -1 marks an unused slot; in each row the used slots come first, at most 64, about a third of them on average; in every draw some partition uses all 64 slots toward a wide neighbour; partitions at narrow index 0 send nothing toward block 3 of a lower neighbour and those at the last narrow index nothing toward a higher one. `edge_sender`: a value below 128 is a local node; 128 + k * 64 + s names slot s of received block k, and only slots that the sending partition uses are named.
All inputs are finite; a program needn't handle non-finite values.
Results may differ from a plain program's by a relative error of at most 0.0085.
Values may be sent and summed in bfloat16 or wider, within the bound.
No kernel may reach another device: no remote copies, remote signals or barrier semaphores. Data moves between devices by JAX's collectives and lax.ppermute only.
A program may use at most 64 MiB of HBM per device.

v0:
```python
import math
import jax
import jax.numpy as jnp
from jax import lax
from jax.sharding import PartitionSpec as P


def shifted(value, axis, steps):
    count = lax.axis_size(axis)
    pairs = [(source, (source + steps) % count) for source in range(count)]
    return lax.ppermute(value, axis, pairs)


def shifted_2(block, axis, distance):
    devices = range(lax.axis_size(axis))
    route = [(i - distance, i) for i in devices if i - distance in devices]
    return lax.ppermute(block, axis, route)


def neighbours(blocks, direction):
    higher = shifted(blocks[0], "wide", direction)
    lower = shifted(blocks[1], "wide", -direction)
    up_side = shifted_2(blocks[2], "narrow", direction)
    down_side = shifted_2(blocks[3], "narrow", -direction)
    return jnp.stack([higher, lower, up_side, down_side], 0)


def norm_parts(second_pre):
    mean_value = jnp.mean(second_pre, -1, keepdims=True)
    centered = second_pre - mean_value
    variance = jnp.mean(centered * centered, -1, keepdims=True)
    inv_std = lax.rsqrt(variance + 1e-05)
    return (centered * inv_std, inv_std)


def clip_share(grad_share, grad_sq, weight_sq, fan_rows):
    unit_ratio = jnp.sqrt((grad_sq + 1e-06) / (weight_sq + 1e-06))
    mean_ratio = jnp.mean(unit_ratio)
    factor = jnp.minimum(
        1.0 / (mean_ratio * jnp.sqrt(weight_sq + 1e-06)), 1.0 / jnp.sqrt(grad_sq + 1e-06)
    )
    return grad_share * factor * math.sqrt(fan_rows)


def edge_contract(hot_table, values):
    return lax.dot_general(
        hot_table,
        values,
        (((0,), (0,)), ((), ())),
        precision=lax.Precision.HIGHEST,
        preferred_element_type=jnp.float32,
    )


def per_device(
    node_latent,
    edge_latent,
    node_cotangent,
    w_first,
    bias_first,
    w_second,
    bias_second,
    norm_gain,
    send_map,
    edge_sender,
    edge_receiver,
):
    node_count, feature_width = node_latent.shape
    halo_slots = send_map.shape[2]
    table_rows = node_count + 4 * halo_slots
    send_hot = (send_map[0][:, :, None] == jnp.arange(node_count, dtype=jnp.int32)).astype(
        jnp.bfloat16
    )
    outgoing = jnp.einsum(
        "khn,nd->khd", send_hot, node_latent, preferred_element_type=jnp.float32
    ).astype(jnp.bfloat16)
    received = neighbours(outgoing, 1)
    node_table = jnp.concatenate([node_latent, received.reshape(4 * halo_slots, feature_width)], 0)
    sender_hot = (edge_sender[:, None] == jnp.arange(table_rows, dtype=jnp.int32)).astype(
        jnp.bfloat16
    )
    receiver_hot = (edge_receiver[:, None] == jnp.arange(node_count, dtype=jnp.int32)).astype(
        jnp.bfloat16
    )
    sender_rows = jnp.dot(sender_hot, node_table, preferred_element_type=jnp.float32).astype(
        jnp.bfloat16
    )
    receiver_rows = jnp.dot(receiver_hot, node_latent, preferred_element_type=jnp.float32).astype(
        jnp.bfloat16
    )
    inputs = jnp.concatenate([edge_latent, sender_rows, receiver_rows], 1)
    preact = jnp.dot(inputs, w_first, preferred_element_type=jnp.float32) + bias_first.astype(
        jnp.float32
    )
    activation = jax.nn.silu(preact).astype(jnp.bfloat16)
    second_pre = jnp.dot(
        activation, w_second, preferred_element_type=jnp.float32
    ) + bias_second.astype(jnp.float32)
    normalized, inv_std = norm_parts(second_pre)
    upstream = jnp.dot(receiver_hot, node_cotangent, preferred_element_type=jnp.float32)
    scaled = upstream * norm_gain.astype(jnp.float32)
    norm_back = (
        inv_std
        * (
            scaled
            - jnp.mean(scaled, -1, keepdims=True)
            - normalized * jnp.mean(scaled * normalized, -1, keepdims=True)
        )
    ).astype(jnp.bfloat16)
    second_grad = lax.dot_general(
        activation, norm_back, (((0,), (0,)), ((), ())), preferred_element_type=jnp.float32
    )
    sigmoid_pre = jax.nn.sigmoid(preact)
    pre_back = (
        jnp.dot(norm_back, w_second.T, preferred_element_type=jnp.float32)
        * sigmoid_pre
        * (1.0 + preact * (1.0 - sigmoid_pre))
    ).astype(jnp.bfloat16)
    first_grad = lax.dot_general(
        inputs, pre_back, (((0,), (0,)), ((), ())), preferred_element_type=jnp.float32
    )
    input_back = jnp.dot(pre_back, w_first.T, preferred_element_type=jnp.float32)
    edge_grad = (upstream + input_back[:, :feature_width]).astype(jnp.bfloat16)
    table_grad = edge_contract(
        sender_hot.astype(jnp.float32), input_back[:, feature_width : 2 * feature_width]
    )
    receiver_grad = edge_contract(
        receiver_hot.astype(jnp.float32), input_back[:, 2 * feature_width :]
    )
    halo_grad = table_grad[node_count:].reshape(4, halo_slots, feature_width).astype(jnp.bfloat16)
    returned = neighbours(halo_grad, -1)
    back = jnp.einsum("khn,khd->nd", send_hot, returned, preferred_element_type=jnp.float32)
    node_grad = (
        node_cotangent.astype(jnp.float32) + table_grad[:node_count] + receiver_grad + back
    ).astype(jnp.bfloat16)
    wide_count = lax.axis_size("wide")
    first_rows = w_first.shape[0] // wide_count
    second_rows = w_second.shape[0] // wide_count
    first_weight_sq = jnp.sum(jnp.square(w_first.astype(jnp.float32)), 0)
    second_weight_sq = jnp.sum(jnp.square(w_second.astype(jnp.float32)), 0)
    first_total, second_total = lax.psum((first_grad, second_grad), ("wide", "narrow"))
    position = lax.axis_index("wide")
    first_share = lax.dynamic_slice_in_dim(first_total, position * first_rows, first_rows, 0)
    second_share = lax.dynamic_slice_in_dim(second_total, position * second_rows, second_rows, 0)
    first_grad_sq = jnp.sum(first_total * first_total, 0)
    second_grad_sq = jnp.sum(second_total * second_total, 0)
    first_update = clip_share(first_share, first_grad_sq, first_weight_sq, w_first.shape[0])
    second_update = clip_share(second_share, second_grad_sq, second_weight_sq, w_second.shape[0])
    return (node_grad, edge_grad, first_update, second_update)


def solution(mesh):
    return jax.shard_map(
        per_device,
        mesh=mesh,
        in_specs=(
            P(("wide", "narrow"), None),
            P(("wide", "narrow"), None),
            P(("wide", "narrow"), None),
            P(),
            P(),
            P(),
            P(),
            P(),
            P(("wide", "narrow"), None, None),
            P(("wide", "narrow")),
            P(("wide", "narrow")),
        ),
        out_specs=(
            P(("wide", "narrow"), None),
            P(("wide", "narrow"), None),
            P("wide", None),
            P("wide", None),
        ),
        check_vma=False,
    )
```

profile of v0, /device:TPU:0, one launch (start us, length us, event | category | flops | bytes accessed | tf_op | source)
XLA Modules:
  0.0 192.4 jit_solution(14532633733271048976)
XLA Ops:
  7.2 0.0 copy-start.4
  7.2 0.0 copy-start.1
  7.2 0.0 all-reduce.3.cloned.1.call-start
  7.2 1.3 convolution_convert_fusion.2
  8.6 1.3 collective-permute-start.3
  9.9 3.0 %collective-permute-start.2 = (bf16[64,512]{1,0:T(8,128)(2,1)S(1)}, bf16[64,512]{1,0:T(8,128)(2,1)S(1)}, u32[]{:S(2)}, u32[]{:S(2)}) collective-permute-start(bf16[64,512]{1,0:T(8,128)(2,1)S(1)} %get-tuple-element.18), channel_id=1, source_target_pairs={{0,1},{2,3},{4,5},{6,7},{8,9},{10,11},{12,13},{14,15},{16,17},{18,... | collective-permute-start | bytes 196616 | tf_op jit(solution)/shard_map/ppermute | solution.py:17
  12.9 7.0 %collective-permute-start.1 = (bf16[64,512]{1,0:T(8,128)(2,1)S(1)}, bf16[64,512]{1,0:T(8,128)(2,1)S(1)}, u32[]{:S(2)}, u32[]{:S(2)}) collective-permute-start(bf16[64,512]{1,0:T(8,128)(2,1)S(1)} %get-tuple-element.19), channel_id=1, source_target_pairs={{0,30},{2,0},{4,2},{6,4},{8,6},{10,8},{12,10},{14,12},{16,14},{18,... | collective-permute-start | bytes 196616 | tf_op jit(solution)/shard_map/ppermute | solution.py:11
  19.9 1.3 convolution_convert_fusion.1
  21.3 0.7 convert_element_type.56
  22.0 0.7 convert_element_type.55
  22.6 1.3 copy.15
  23.9 0.7 convert_element_type.53
  24.6 3.2 %collective-permute-done = bf16[64,512]{1,0:T(8,128)(2,1)S(1)} collective-permute-done((bf16[64,512]{1,0:T(8,128)(2,1)S(1)}, bf16[64,512]{1,0:T(8,128)(2,1)S(1)}, u32[]{:S(2)}, u32[]{:S(2)}) %collective-permute-start) | collective-permute-done | bytes 65568 | tf_op jit(solution)/shard_map/ppermute | solution.py:11
  27.9 0.6 convolution_convert_fusion
  28.5 0.0 copy-start.5
  28.5 1.0 convolution_add_fusion.1
  29.5 0.0 copy-done.5
  29.5 0.6 fusion.33
  30.2 0.2 multiply_reduce_fusion.5
  30.4 0.1 copy-done.6
  30.4 0.5 multiply_reduce_fusion.6
  31.0 0.3 multiply_convert_fusion
  31.3 0.7 fusion.1
  31.9 0.1 copy-done
  32.0 1.5 fusion.31
  33.5 2.7 %fusion.7 = f32[1536,512]{1,0:T(8,128)} fusion(bf16[512,512]{1,0:T(8,128)(2,1)S(1)} %fusion.1, bf16[512,512]{0,1:T(8,128)(2,1)S(1)} %convolution_convert_fusion.1, bf16[512,512]{0,1:T(8,128)(2,1)S(1)} %convolution_convert_fusion, bf16[512,512]{0,1:T(8,128)(2,1)S(1)} %copy.15), kind=kOutput, calls=%fused_computation.28 | convolution fusion | flops 810024960 | bytes 5242880 | tf_op jit(solution)/shard_map/dot_general | solution.py:119
  36.2 0.0 all-reduce.3.cloned.1.call-update
  36.2 0.2 multiply_reduce_fusion.2
  36.4 0.4 multiply_reduce_fusion
  36.8 2.6 %fusion.35 = f32[512,1536]{1,0:T(8,128)S(1)} fusion(bf16[512,512]{1,0:T(8,128)(2,1)} %copy-done.3, bf16[1536,512]{1,0:T(8,128)(2,1)} %param.14), kind=kOutput, calls=%fused_computation.74 | convolution fusion | flops 805306368 | bytes 5242880 | tf_op jit(solution)/shard_map/dot_general | solution.py:122
  39.3 1.0 slice.69
  40.4 1.8 fusion.34
  42.3 1.9 collective-permute-start.7
  44.2 1.3 collective-permute-start.6
  45.5 0.1 collective-permute-start.5
  45.5 5.6 %collective-permute-start.4 = (bf16[64,512]{1,0:T(8,128)(2,1)S(1)}, bf16[64,512]{1,0:T(8,128)(2,1)}, u32[]{:S(2)}, u32[]{:S(2)}) collective-permute-start(bf16[64,512]{1,0:T(8,128)(2,1)S(1)} %get-tuple-element.12), channel_id=1, source_target_pairs={{0,30},{2,0},{4,2},{6,4},{8,6},{10,8},{12,10},{14,12},{16,14},{18,... | collective-permute-start | bytes 196616 | tf_op jit(solution)/shard_map/ppermute | solution.py:11
  51.1 2.6 %copy.18 = f32[512,512]{0,1:T(8,128)} copy(f32[512,512]{1,0:T(8,128)} %slice.69) | data formatting | bytes 2097152
  53.7 2.6 %add_convert_fusion = bf16[512,512]{0,1:T(8,128)(2,1)} fusion(f32[512,512]{0,1:T(8,128)} %copy-done, f32[512,512]{0,1:T(8,128)} %copy.18), kind=kLoop, calls=%fused_computation.20 | loop fusion | flops 524288 | bytes 2621440 | tf_op jit(solution)/shard_map/convert_element_type | solution.py:123
  56.2 2.3 %convolution_add_fusion.2 = f32[128,512]{1,0:T(8,128)} fusion(f32[512,1536]{1,0:T(8,128)S(1)} %fusion.35, f32[384,512]{1,0:T(8,128)} %get-tuple-element.24, bf16[128,512]{1,0:T(8,128)(2,1)S(1)} %copy-done.6, s32[512]{0:T(512)S(1)} %copy-done.7), kind=kOutput, calls=%fused_computation.12 | convolution fusion | flops 402915328 | bytes 1705984 | tf_op jit(solution)/shard_map/dot_general | solution.py:46
  58.5 2.0 %copy.17 = bf16[512,512]{1,0:T(8,128)(2,1)} copy(bf16[512,512]{0,1:T(8,128)(2,1)} %add_convert_fusion) | data formatting | bytes 1048576
  60.6 2.0 %fusion.3 = bf16[128,512]{1,0:T(8,128)(2,1)} fusion(f32[128,512]{1,0:T(8,128)} %convolution_add_fusion.2, bf16[1,64,512]{2,1,0:T(8,128)(2,1)} %bitcast.14, bf16[1,64,512]{2,1,0:T(8,128)(2,1)} %bitcast.13, bf16[1,64,512]{2,1,0:T(8,128)(2,1)} %bitcast.12, bf16[1,64,512]{2,1,0:T(8,128)(2,1)} %bitcast.11, s32[4,64]{1,0:T(4,128)S(1)} %bitcast.43), kind=kOutput, calls=%fused_computation.14 | convolution fusion | flops 34111488 | bytes 656384 | tf_op jit(solution)/shard_map/khn,khd->nd/dot_general | solution.py:132
  62.6 115.6 %all-reduce.3.cloned.1.call-done = (f32[1536,512]{1,0:T(8,128)}, f32[512,512]{1,0:T(8,128)}) async-done(((f32[1536,512]{1,0:T(8,128)}, f32[512,512]{1,0:T(8,128)}), (f32[1536,512]{1,0:T(8,128)}, f32[512,512]{1,0:T(8,128)})) %all-reduce.3.cloned.1.call-update) | async-done | bytes 4194320 | tf_op jit(solution)/shard_map/psum | solution.py:141
  178.3 2.3 %multiply_reduce_fusion.1 = f32[512]{0:T(512)S(1)} fusion(f32[1536,512]{1,0:T(8,128)} %get-tuple-element.10), kind=kLoop, calls=%fused_computation.1 | loop fusion | flops 1572352 | bytes 3147776 | tf_op jit(solution)/shard_map/reduce_sum | solution.py:145
  180.5 0.6 sqrt_reduce_fusion.1
  181.8 0.1 multiply_reduce_fusion.3
  182.0 0.6 sqrt_reduce_fusion
  183.2 1.6 multiply_multiply_fusion
  184.9 0.6 multiply_multiply_fusion.1
  (30 shorter events, 0.2 us)
Async XLA Ops:
  7.2 20.7 %copy-start.4 = (bf16[128,512]{1,0:T(8,128)(2,1)S(1)}, bf16[128,512]{1,0:T(8,128)(2,1)}, u32[]{:S(2)}) copy-start(bf16[128,512]{1,0:T(8,128)(2,1)} %param.11) | copy-start | bytes 393220
  7.2 20.7 %copy-start.8 = (s32[512]{0:T(512)S(1)}, s32[512]{0:T(512)}, u32[]{:S(2)}) copy-start(s32[512]{0:T(512)} %param.20) | copy-start | bytes 6148
  7.2 21.3 %copy-start.1 = (bf16[1536,512]{1,0:T(8,128)(2,1)S(1)}, bf16[1536,512]{1,0:T(8,128)(2,1)}, u32[]{:S(2)}) copy-start(bf16[1536,512]{1,0:T(8,128)(2,1)} %param.14) | copy-start | bytes 4718596
  7.2 171.1 %all-reduce.3.cloned.1.call-start = ((), (), s32[]{:S(2)}) async-start(), calls=%async_computation | async-start | bytes 8388608 | tf_op jit(solution)/shard_map/psum | solution.py:141
  8.6 16.0 %collective-permute-start.3 = (bf16[64,512]{1,0:T(8,128)(2,1)S(1)}, bf16[64,512]{1,0:T(8,128)(2,1)S(1)}, u32[]{:S(2)}, u32[]{:S(2)}) collective-permute-start(bf16[64,512]{1,0:T(8,128)(2,1)S(1)} %get-tuple-element.17), channel_id=1, source_target_pairs={{1,0},{3,2},{5,4},{7,6},{9,8},{11,10},{13,12},{15,14},{17,16},{19,... | collective-permute-start | bytes 196616 | tf_op jit(solution)/shard_map/ppermute | solution.py:17
  9.9 14.7 %collective-permute-start.2 = (bf16[64,512]{1,0:T(8,128)(2,1)S(1)}, bf16[64,512]{1,0:T(8,128)(2,1)S(1)}, u32[]{:S(2)}, u32[]{:S(2)}) collective-permute-start(bf16[64,512]{1,0:T(8,128)(2,1)S(1)} %get-tuple-element.18), channel_id=1, source_target_pairs={{0,1},{2,3},{4,5},{6,7},{8,9},{10,11},{12,13},{14,15},{16,17},{18,... | collective-permute-start | bytes 196616 | tf_op jit(solution)/shard_map/ppermute | solution.py:17
  12.9 11.7 %collective-permute-start.1 = (bf16[64,512]{1,0:T(8,128)(2,1)S(1)}, bf16[64,512]{1,0:T(8,128)(2,1)S(1)}, u32[]{:S(2)}, u32[]{:S(2)}) collective-permute-start(bf16[64,512]{1,0:T(8,128)(2,1)S(1)} %get-tuple-element.19), channel_id=1, source_target_pairs={{0,30},{2,0},{4,2},{6,4},{8,6},{10,8},{12,10},{14,12},{16,14},{18,... | collective-permute-start | bytes 196616 | tf_op jit(solution)/shard_map/ppermute | solution.py:11
  19.9 7.9 %collective-permute-start = (bf16[64,512]{1,0:T(8,128)(2,1)S(1)}, bf16[64,512]{1,0:T(8,128)(2,1)S(1)}, u32[]{:S(2)}, u32[]{:S(2)}) collective-permute-start(bf16[64,512]{1,0:T(8,128)(2,1)S(1)} %get-tuple-element.16), channel_id=1, source_target_pairs={{0,2},{2,4},{4,6},{6,8},{8,10},{10,12},{12,14},{14,16},{16,18},{18... | collective-permute-start | bytes 196616 | tf_op jit(solution)/shard_map/ppermute | solution.py:11
  28.5 1.0 copy-start.5
  29.5 0.9 copy-start.6
  29.5 0.9 copy-start.7
  30.9 1.1 copy-start
  32.0 1.5 copy-start.3
  42.3 18.3 %collective-permute-start.7 = (bf16[64,512]{1,0:T(8,128)(2,1)S(1)}, bf16[64,512]{1,0:T(8,128)(2,1)}, u32[]{:S(2)}, u32[]{:S(2)}) collective-permute-start(bf16[64,512]{1,0:T(8,128)(2,1)S(1)} %get-tuple-element.13), channel_id=1, source_target_pairs={{0,1},{2,3},{4,5},{6,7},{8,9},{10,11},{12,13},{14,15},{16,17},{18,... | collective-permute-start | bytes 196616 | tf_op jit(solution)/shard_map/ppermute | solution.py:17
  44.2 16.4 %collective-permute-start.6 = (bf16[64,512]{1,0:T(8,128)(2,1)S(1)}, bf16[64,512]{1,0:T(8,128)(2,1)}, u32[]{:S(2)}, u32[]{:S(2)}) collective-permute-start(bf16[64,512]{1,0:T(8,128)(2,1)S(1)} %get-tuple-element.14), channel_id=1, source_target_pairs={{1,0},{3,2},{5,4},{7,6},{9,8},{11,10},{13,12},{15,14},{17,16},{19,... | collective-permute-start | bytes 196616 | tf_op jit(solution)/shard_map/ppermute | solution.py:17
  45.5 15.1 %collective-permute-start.5 = (bf16[64,512]{1,0:T(8,128)(2,1)S(1)}, bf16[64,512]{1,0:T(8,128)(2,1)}, u32[]{:S(2)}, u32[]{:S(2)}) collective-permute-start(bf16[64,512]{1,0:T(8,128)(2,1)S(1)} %get-tuple-element.15), channel_id=1, source_target_pairs={{0,2},{2,4},{4,6},{6,8},{8,10},{10,12},{12,14},{14,16},{16,18},{18... | collective-permute-start | bytes 196616 | tf_op jit(solution)/shard_map/ppermute | solution.py:11
  45.5 15.0 %collective-permute-start.4 = (bf16[64,512]{1,0:T(8,128)(2,1)S(1)}, bf16[64,512]{1,0:T(8,128)(2,1)}, u32[]{:S(2)}, u32[]{:S(2)}) collective-permute-start(bf16[64,512]{1,0:T(8,128)(2,1)S(1)} %get-tuple-element.12), channel_id=1, source_target_pairs={{0,30},{2,0},{4,2},{6,4},{8,6},{10,8},{12,10},{14,12},{16,14},{18,... | collective-permute-start | bytes 196616 | tf_op jit(solution)/shard_map/ppermute | solution.py:11
  53.7 6.9 %copy-start.9 = (s32[1,4,64]{2,1,0:T(4,128)S(1)}, s32[1,4,64]{2,1,0:T(4,128)}, u32[]{:S(2)}) copy-start(s32[1,4,64]{2,1,0:T(4,128)} %param.19) | copy-start | bytes 3076
  178.3 3.5 %copy-start.2 = (f32[512,512]{1,0:T(8,128)S(1)}, f32[512,512]{1,0:T(8,128)}, u32[]{:S(2)}) copy-start(f32[512,512]{1,0:T(8,128)} %get-tuple-element.11) | copy-start | bytes 3145732
Sparse Core Ops, SparseCore 0:
  36.3 141.9 all-reduce.2
where the time goes:
time: 193 us; the launch traced here: 192 us
  waiting for transfers between devices  119 us (62%)
  starting transfers between devices  20.2 us (10%)
  matrix products  18.9 us (10%)
  between operations  15.6 us (8%)
  other arithmetic  11.6 us (6%)
  local copies, waits for them, and re-layouts  7.15 us (4%)
    psum x1, waiting for transfers between devices, per_device(): lax.psum((first_grad, second_grad), ('wide', 'narrow'))  116 us
    ppermute x4, starting transfers between devices, shifted(): return lax.ppermute(value, axis, pairs)  12.7 us
    ppermute x4, starting transfers between devices, shifted_2(): return lax.ppermute(block, axis, route)  7.52 us
    unnamed x23, local copies, waits for them, and re-layouts  6.07 us
    dot_general x2, matrix products, edge_contract(): lax.dot_general(hot_table, values, (((0,), (0,)), ((), ())), precision=la...  4.11 us
  transfers between devices with their start and end apart: 9, of which 2 were waited for; matrix products, arithmetic and copies ran while one was open for 12% of the time, Pallas kernels for 0%

commit v1 on v0

--- a/solution.py
+++ b/solution.py
@@ -138,7 +138,7 @@
     second_rows = w_second.shape[0] // wide_count
     first_weight_sq = jnp.sum(jnp.square(w_first.astype(jnp.float32)), 0)
     second_weight_sq = jnp.sum(jnp.square(w_second.astype(jnp.float32)), 0)
-    first_total, second_total = lax.psum((first_grad, second_grad), ("wide", "narrow"))
+    first_total, second_total = lax.psum(lax.psum((first_grad, second_grad), "wide"), "narrow")
     position = lax.axis_index("wide")
     first_share = lax.dynamic_slice_in_dim(first_total, position * first_rows, first_rows, 0)
     second_share = lax.dynamic_slice_in_dim(second_total, position * second_rows, second_rows, 0)

time: 193 us -> 247 us (1.28)
  waiting for transfers between devices: 119 us -> 173 us
    psum x1 -> x2, waiting for transfers between devices: 116 us -> 170 us  [the longest x1 167 us: per_device(): lax.psum((first_grad, second_grad), 'wide')]
  transfers between devices with their start and end apart: 9 -> 10, of which waited for: 2 -> 3; matrix products, arithmetic and copies ran while one was open for 12% -> 9% of each run, Pallas kernels for 0% -> 0%
where the time goes in v1:
time: 247 us
  waiting for transfers between devices  173 us (70%)
  starting transfers between devices  20.4 us (8%)
  matrix products  19 us (8%)
  between operations  15.6 us (6%)
  other arithmetic  11.5 us (5%)
  local copies, waits for them, and re-layouts  7.17 us (3%)
    psum x1, waiting for transfers between devices, per_device(): lax.psum((first_grad, second_grad), 'wide')  167 us
    ppermute x4, starting transfers between devices, shifted(): return lax.ppermute(value, axis, pairs)  12.7 us
    ppermute x4, starting transfers between devices, shifted_2(): return lax.ppermute(block, axis, route)  7.63 us
    unnamed x23, local copies, waits for them, and re-layouts  6.09 us
  transfers between devices with their start and end apart: 10, of which 3 were waited for; matrix products, arithmetic and copies ran while one was open for 9% of the time, Pallas kernels for 0%

profile of v1, /device:TPU:0, one launch (start us, length us, event | category | flops | bytes accessed | tf_op | source)
XLA Modules:
  0.0 246.8 jit_solution(4955441316672108275)
XLA Ops:
  7.2 0.0 all-reduce.5.cloned.1.call-start
  7.2 1.3 convolution_convert_fusion.2
  8.6 1.3 collective-permute-start.3
  9.9 3.0 %collective-permute-start.2 = (bf16[64,512]{1,0:T(8,128)(2,1)S(1)}, bf16[64,512]{1,0:T(8,128)(2,1)S(1)}, u32[]{:S(2)}, u32[]{:S(2)}) collective-permute-start(bf16[64,512]{1,0:T(8,128)(2,1)S(1)} %get-tuple-element.20), channel_id=1, source_target_pairs={{0,1},{2,3},{4,5},{6,7},{8,9},{10,11},{12,13},{14,15},{16,17},{18,... | collective-permute-start | bytes 196616 | tf_op jit(solution)/shard_map/ppermute | solution.py:17
  12.9 7.0 %collective-permute-start.1 = (bf16[64,512]{1,0:T(8,128)(2,1)S(1)}, bf16[64,512]{1,0:T(8,128)(2,1)S(1)}, u32[]{:S(2)}, u32[]{:S(2)}) collective-permute-start(bf16[64,512]{1,0:T(8,128)(2,1)S(1)} %get-tuple-element.21), channel_id=1, source_target_pairs={{0,30},{2,0},{4,2},{6,4},{8,6},{10,8},{12,10},{14,12},{16,14},{18,... | collective-permute-start | bytes 196616 | tf_op jit(solution)/shard_map/ppermute | solution.py:11
  19.9 1.3 convolution_convert_fusion.1
  21.3 0.7 convert_element_type.56
  22.0 0.7 convert_element_type.55
  22.6 1.3 copy.15
  23.9 0.7 convert_element_type.53
  24.6 3.2 %collective-permute-done = bf16[64,512]{1,0:T(8,128)(2,1)S(1)} collective-permute-done((bf16[64,512]{1,0:T(8,128)(2,1)S(1)}, bf16[64,512]{1,0:T(8,128)(2,1)S(1)}, u32[]{:S(2)}, u32[]{:S(2)}) %collective-permute-start) | collective-permute-done | bytes 65568 | tf_op jit(solution)/shard_map/ppermute | solution.py:11
  27.9 0.6 convolution_convert_fusion
  28.5 1.0 convolution_add_fusion.1
  29.5 0.0 copy-done.5
  29.5 0.6 fusion.33
  30.2 0.2 multiply_reduce_fusion.5
  30.4 0.1 copy-done.6
  30.4 0.5 multiply_reduce_fusion.6
  31.0 0.3 multiply_convert_fusion
  31.3 0.7 fusion.1
  31.9 0.1 copy-done
  32.0 1.5 fusion.31
  33.5 2.7 %fusion.7 = f32[1536,512]{1,0:T(8,128)} fusion(bf16[512,512]{1,0:T(8,128)(2,1)S(1)} %fusion.1, bf16[512,512]{0,1:T(8,128)(2,1)S(1)} %convolution_convert_fusion.1, bf16[512,512]{0,1:T(8,128)(2,1)S(1)} %convolution_convert_fusion, bf16[512,512]{0,1:T(8,128)(2,1)S(1)} %copy.15), kind=kOutput, calls=%fused_computation.28 | convolution fusion | flops 810024960 | bytes 5242880 | tf_op jit(solution)/shard_map/dot_general | solution.py:119
  36.2 0.0 all-reduce.5.cloned.1.call-update
  36.2 0.0 all-reduce.7.cloned.1.call-start
  36.2 166.6 %all-reduce.5.cloned.1.call-done = (f32[1536,512]{1,0:T(8,128)}, f32[512,512]{1,0:T(8,128)}) async-done(((f32[1536,512]{1,0:T(8,128)}, f32[512,512]{1,0:T(8,128)}), (f32[1536,512]{1,0:T(8,128)}, f32[512,512]{1,0:T(8,128)})) %all-reduce.5.cloned.1.call-update) | async-done | bytes 4194320 | tf_op jit(solution)/shard_map/psum | solution.py:141
  202.9 0.0 all-reduce.7.cloned.1.call-update
  202.9 0.2 multiply_reduce_fusion.2
  203.1 0.4 multiply_reduce_fusion
  203.5 2.6 %fusion.35 = f32[512,1536]{1,0:T(8,128)S(1)} fusion(bf16[512,512]{1,0:T(8,128)(2,1)} %copy-done.3, bf16[1536,512]{1,0:T(8,128)(2,1)} %param.14), kind=kOutput, calls=%fused_computation.74 | convolution fusion | flops 805306368 | bytes 5242880 | tf_op jit(solution)/shard_map/dot_general | solution.py:122
  206.1 1.0 slice.69
  207.1 1.8 fusion.34
  209.0 2.0 collective-permute-start.7
  211.0 1.3 collective-permute-start.6
  212.3 1.5 collective-permute-start.5
  213.8 4.2 %collective-permute-start.4 = (bf16[64,512]{1,0:T(8,128)(2,1)S(1)}, bf16[64,512]{1,0:T(8,128)(2,1)}, u32[]{:S(2)}, u32[]{:S(2)}) collective-permute-start(bf16[64,512]{1,0:T(8,128)(2,1)S(1)} %get-tuple-element.14), channel_id=1, source_target_pairs={{0,30},{2,0},{4,2},{6,4},{8,6},{10,8},{12,10},{14,12},{16,14},{18,... | collective-permute-start | bytes 196616 | tf_op jit(solution)/shard_map/ppermute | solution.py:11
  218.0 2.5 %copy.18 = f32[512,512]{0,1:T(8,128)} copy(f32[512,512]{1,0:T(8,128)} %slice.69) | data formatting | bytes 2097152
  220.5 2.5 %add_convert_fusion = bf16[512,512]{0,1:T(8,128)(2,1)} fusion(f32[512,512]{0,1:T(8,128)} %copy-done, f32[512,512]{0,1:T(8,128)} %copy.18), kind=kLoop, calls=%fused_computation.20 | loop fusion | flops 524288 | bytes 2621440 | tf_op jit(solution)/shard_map/convert_element_type | solution.py:123
  223.0 2.3 convolution_add_fusion.2
  225.3 2.1 copy.17
  227.4 2.1 fusion.3
  229.5 3.3 %all-reduce.7.cloned.1.call-done = (f32[1536,512]{1,0:T(8,128)}, f32[512,512]{1,0:T(8,128)}) async-done(((f32[1536,512]{1,0:T(8,128)}, f32[512,512]{1,0:T(8,128)}), (f32[1536,512]{1,0:T(8,128)}, f32[512,512]{1,0:T(8,128)})) %all-reduce.7.cloned.1.call-update) | async-done | bytes 4194320 | tf_op jit(solution)/shard_map/psum | solution.py:141
  232.8 2.3 multiply_reduce_fusion.1
  235.0 0.6 sqrt_reduce_fusion.1
  236.3 0.1 multiply_reduce_fusion.3
  236.4 0.6 sqrt_reduce_fusion
  237.7 1.6 multiply_multiply_fusion
  239.4 0.6 multiply_multiply_fusion.1
  (33 shorter events, 0.2 us)
Async XLA Ops:
  7.2 20.7 %copy-start.4 = (bf16[128,512]{1,0:T(8,128)(2,1)S(1)}, bf16[128,512]{1,0:T(8,128)(2,1)}, u32[]{:S(2)}) copy-start(bf16[128,512]{1,0:T(8,128)(2,1)} %param.11) | copy-start | bytes 393220
  7.2 20.7 %copy-start.8 = (s32[512]{0:T(512)S(1)}, s32[512]{0:T(512)}, u32[]{:S(2)}) copy-start(s32[512]{0:T(512)} %param.20) | copy-start | bytes 6148
  7.2 21.3 %copy-start.1 = (bf16[1536,512]{1,0:T(8,128)(2,1)S(1)}, bf16[1536,512]{1,0:T(8,128)(2,1)}, u32[]{:S(2)}) copy-start(bf16[1536,512]{1,0:T(8,128)(2,1)} %param.14) | copy-start | bytes 4718596
  7.2 195.7 %all-reduce.5.cloned.1.call-start = ((), (), s32[]{:S(2)}) async-start(), calls=%async_computation | async-start | bytes 8388608 | tf_op jit(solution)/shard_map/psum | solution.py:141
  8.6 16.0 %collective-permute-start.3 = (bf16[64,512]{1,0:T(8,128)(2,1)S(1)}, bf16[64,512]{1,0:T(8,128)(2,1)S(1)}, u32[]{:S(2)}, u32[]{:S(2)}) collective-permute-start(bf16[64,512]{1,0:T(8,128)(2,1)S(1)} %get-tuple-element.19), channel_id=1, source_target_pairs={{1,0},{3,2},{5,4},{7,6},{9,8},{11,10},{13,12},{15,14},{17,16},{19,... | collective-permute-start | bytes 196616 | tf_op jit(solution)/shard_map/ppermute | solution.py:17
  9.9 14.7 %collective-permute-start.2 = (bf16[64,512]{1,0:T(8,128)(2,1)S(1)}, bf16[64,512]{1,0:T(8,128)(2,1)S(1)}, u32[]{:S(2)}, u32[]{:S(2)}) collective-permute-start(bf16[64,512]{1,0:T(8,128)(2,1)S(1)} %get-tuple-element.20), channel_id=1, source_target_pairs={{0,1},{2,3},{4,5},{6,7},{8,9},{10,11},{12,13},{14,15},{16,17},{18,... | collective-permute-start | bytes 196616 | tf_op jit(solution)/shard_map/ppermute | solution.py:17
  12.9 11.7 %collective-permute-start.1 = (bf16[64,512]{1,0:T(8,128)(2,1)S(1)}, bf16[64,512]{1,0:T(8,128)(2,1)S(1)}, u32[]{:S(2)}, u32[]{:S(2)}) collective-permute-start(bf16[64,512]{1,0:T(8,128)(2,1)S(1)} %get-tuple-element.21), channel_id=1, source_target_pairs={{0,30},{2,0},{4,2},{6,4},{8,6},{10,8},{12,10},{14,12},{16,14},{18,... | collective-permute-start | bytes 196616 | tf_op jit(solution)/shard_map/ppermute | solution.py:11
  19.9 7.9 %collective-permute-start = (bf16[64,512]{1,0:T(8,128)(2,1)S(1)}, bf16[64,512]{1,0:T(8,128)(2,1)S(1)}, u32[]{:S(2)}, u32[]{:S(2)}) collective-permute-start(bf16[64,512]{1,0:T(8,128)(2,1)S(1)} %get-tuple-element.18), channel_id=1, source_target_pairs={{0,2},{2,4},{4,6},{6,8},{8,10},{10,12},{12,14},{14,16},{16,18},{18... | collective-permute-start | bytes 196616 | tf_op jit(solution)/shard_map/ppermute | solution.py:11
  28.5 1.0 copy-start.5
  29.5 0.9 copy-start.6
  29.5 0.9 copy-start.7
  30.9 1.1 copy-start
  32.0 1.5 copy-start.3
  36.2 196.6 %all-reduce.7.cloned.1.call-start = ((), (), s32[]{:S(2)}) async-start(), calls=%async_computation.1 | async-start | bytes 8388608 | tf_op jit(solution)/shard_map/psum | solution.py:141
  209.0 18.4 %collective-permute-start.7 = (bf16[64,512]{1,0:T(8,128)(2,1)S(1)}, bf16[64,512]{1,0:T(8,128)(2,1)}, u32[]{:S(2)}, u32[]{:S(2)}) collective-permute-start(bf16[64,512]{1,0:T(8,128)(2,1)S(1)} %get-tuple-element.15), channel_id=1, source_target_pairs={{0,1},{2,3},{4,5},{6,7},{8,9},{10,11},{12,13},{14,15},{16,17},{18,... | collective-permute-start | bytes 196616 | tf_op jit(solution)/shard_map/ppermute | solution.py:17
  211.0 16.4 %collective-permute-start.6 = (bf16[64,512]{1,0:T(8,128)(2,1)S(1)}, bf16[64,512]{1,0:T(8,128)(2,1)}, u32[]{:S(2)}, u32[]{:S(2)}) collective-permute-start(bf16[64,512]{1,0:T(8,128)(2,1)S(1)} %get-tuple-element.16), channel_id=1, source_target_pairs={{1,0},{3,2},{5,4},{7,6},{9,8},{11,10},{13,12},{15,14},{17,16},{19,... | collective-permute-start | bytes 196616 | tf_op jit(solution)/shard_map/ppermute | solution.py:17
  212.3 15.1 %collective-permute-start.5 = (bf16[64,512]{1,0:T(8,128)(2,1)S(1)}, bf16[64,512]{1,0:T(8,128)(2,1)}, u32[]{:S(2)}, u32[]{:S(2)}) collective-permute-start(bf16[64,512]{1,0:T(8,128)(2,1)S(1)} %get-tuple-element.17), channel_id=1, source_target_pairs={{0,2},{2,4},{4,6},{6,8},{8,10},{10,12},{12,14},{14,16},{16,18},{18... | collective-permute-start | bytes 196616 | tf_op jit(solution)/shard_map/ppermute | solution.py:11
  213.8 13.6 %collective-permute-start.4 = (bf16[64,512]{1,0:T(8,128)(2,1)S(1)}, bf16[64,512]{1,0:T(8,128)(2,1)}, u32[]{:S(2)}, u32[]{:S(2)}) collective-permute-start(bf16[64,512]{1,0:T(8,128)(2,1)S(1)} %get-tuple-element.14), channel_id=1, source_target_pairs={{0,30},{2,0},{4,2},{6,4},{8,6},{10,8},{12,10},{14,12},{16,14},{18,... | collective-permute-start | bytes 196616 | tf_op jit(solution)/shard_map/ppermute | solution.py:11
  220.5 6.9 %copy-start.9 = (s32[1,4,64]{2,1,0:T(4,128)S(1)}, s32[1,4,64]{2,1,0:T(4,128)}, u32[]{:S(2)}) copy-start(s32[1,4,64]{2,1,0:T(4,128)} %param.19) | copy-start | bytes 3076
  232.8 3.5 %copy-start.2 = (f32[512,512]{1,0:T(8,128)S(1)}, f32[512,512]{1,0:T(8,128)}, u32[]{:S(2)}) copy-start(f32[512,512]{1,0:T(8,128)} %get-tuple-element.13) | copy-start | bytes 3145732
Sparse Core Ops, SparseCore 0:
  36.3 166.5 all-reduce.4
  205.4 27.3 all-reduce.6
